TPU v7x, 512 devices: a whole 4x4x16 slice. The times are simulated.
512 devices in a mesh: dp: 8 (over y, core), expert: 64 (over z, x).
Axes of the slice: x: 4, y: 4, z: 16, core: 2. Of those that a mesh axis runs over, the one named last changes fastest.
Arguments:
- tokens: bfloat16 [65536, 1920], P(('dp', 'expert')), may hold values from -10 to 10
- assignment: int32 [65536], P(('dp', 'expert')), may hold values from 0 to 63, as said below
- centroids: bfloat16 [64, 1920], P('expert'), may hold values from -0.125 to 0.125
- norm_gain: float32 [64, 1920], P('expert'), may hold values from 0.25 to 1.75
- inner_weight: bfloat16 [64, 4096, 1920], P('expert', 'dp'), may hold values from -0.125 to 0.125
- outer_weight: bfloat16 [64, 4096, 1920], P('expert', 'dp'), may hold values from -0.09375 to 0.09375
Outputs:
- layer_out: bfloat16 [65536, 1920], P(('dp', 'expert'))
Inputs may be any that keep to these rules, and one draw needn't show every extreme that they name: `assignment`: each expert is assigned exactly 128 of the tokens of the devices that share one index of dp. One device assigns at most 4 of its tokens to one expert, and every expert gets exactly 4 tokens from some device of each index of dp.
All inputs are finite; a program needn't handle non-finite values.
Results may differ from a plain program's by a relative error of at most 0.007.
Values may be sent and summed in bfloat16 or wider, within the bound.
A program may use at most 64 MiB of HBM per device.

v0:
```python
import jax
import jax.numpy as jnp
from jax import lax
from jax.sharding import PartitionSpec as P

epsilon = 1e-05


def in_one_piece(arrays, axis, split_dim, concat_dim, along):
    columns = [a.reshape(*a.shape[:along], -1) for a in arrays]
    both = jnp.concatenate(columns, axis=along)
    out, at, done = (
        lax.all_to_all(both, axis, split_axis=split_dim, concat_axis=concat_dim, tiled=True),
        0,
        [],
    )
    for a, column in zip(arrays, columns):
        slab = out[..., at : at + column.shape[along]]
        done.append(slab.reshape(*slab.shape[:along], *a.shape[along:]))
        at += column.shape[along]
    return tuple(done)


def normalize(rows_in, gain_row):
    values = rows_in.astype(jnp.float32)
    center = jnp.mean(values, axis=1, keepdims=True)
    spread = jnp.mean(jnp.square(values - center), axis=1, keepdims=True)
    return ((values - center) * lax.rsqrt(spread + epsilon) * gain_row).astype(jnp.bfloat16)


def expert_rows(normed, inner_mat, outer_mat):
    inner_act = lax.dot_general(
        normed, inner_mat, (((1,), (1,)), ((), ())), preferred_element_type=jnp.float32
    )
    hidden = jnp.maximum(inner_act, 0.0).astype(jnp.bfloat16)
    return jnp.dot(hidden, outer_mat, preferred_element_type=jnp.float32)


def body(tokens, assignment, centroids, norm_gain, inner_weight, outer_weight):
    tok_count = tokens.shape[0]
    experts = lax.axis_size("expert")
    capacity = 2 * tok_count // experts
    slot_total = experts * capacity
    expert_ids = jnp.arange(experts, dtype=jnp.int32)
    token_ids = jnp.arange(tok_count, dtype=jnp.int32)
    slot_ids = jnp.arange(slot_total, dtype=jnp.int32)
    onehot = (assignment[:, None] == expert_ids[None, :]).astype(jnp.int32)
    before = jnp.cumsum(onehot, axis=0) - onehot
    position = jnp.sum(before * onehot, axis=1)
    send_counts = jnp.sum(onehot, axis=0)
    slot_of = assignment * capacity + position
    matches = slot_of[None, :] == slot_ids[:, None]
    occupied = jnp.any(matches, axis=1)
    source_row = jnp.sum(jnp.where(matches, token_ids[None, :], 0), axis=1)
    outgoing = jnp.where(
        occupied[:, None], jnp.take(tokens, source_row, axis=0), jnp.zeros((), jnp.bfloat16)
    )
    arrived, arrived_counts = (
        lax.all_to_all(outgoing, "expert", split_axis=0, concat_axis=0, tiled=True),
        lax.all_to_all(send_counts, "expert", split_axis=0, concat_axis=0, tiled=True),
    )
    inclusive = jnp.cumsum(arrived_counts)
    offsets = inclusive - arrived_counts
    sender = jnp.sum((inclusive[None, :] <= token_ids[:, None]).astype(jnp.int32), axis=1)
    within = token_ids - offsets[sender]
    local_rows = jnp.take(arrived, sender * capacity + within, axis=0)
    inner_mat = inner_weight[0]
    outer_mat = outer_weight[0]
    partial_value = expert_rows(
        normalize(lax.all_gather(local_rows, "dp", axis=0, tiled=True), norm_gain),
        inner_mat,
        outer_mat,
    )
    expert_out = lax.psum_scatter(
        partial_value.astype(jnp.bfloat16), "dp", scatter_dimension=0, tiled=True
    )
    slot_sender = slot_ids // capacity
    slot_within = slot_ids % capacity
    slot_live = slot_within < arrived_counts[slot_sender]
    compact = jnp.where(slot_live, offsets[slot_sender] + slot_within, 0)
    returning = jnp.where(
        slot_live[:, None], jnp.take(expert_out, compact, axis=0), jnp.zeros((), jnp.bfloat16)
    )
    local_score = jnp.dot(local_rows, centroids[0], preferred_element_type=jnp.float32)
    local_gate = jax.nn.sigmoid(local_score).astype(jnp.bfloat16)
    gate_slots = jnp.where(slot_live, jnp.take(local_gate, compact), jnp.zeros((), jnp.bfloat16))
    back_rows, back_gate = in_one_piece((returning, gate_slots), "expert", 0, 0, 1)
    gate_value = jnp.take(back_gate, slot_of)
    combined = jnp.take(back_rows, slot_of, axis=0)
    mixed_out = tokens.astype(jnp.float32) + gate_value.astype(jnp.float32)[
        :, None
    ] * combined.astype(jnp.float32)
    return mixed_out.astype(jnp.bfloat16)


def solution(mesh):
    in_specs = (
        P(("dp", "expert"), None),
        P(("dp", "expert")),
        P("expert", None),
        P("expert", None),
        P("expert", "dp", None),
        P("expert", "dp", None),
    )
    out_specs = P(("dp", "expert"), None)
    return jax.shard_map(body, mesh=mesh, in_specs=in_specs, out_specs=out_specs, check_vma=False)
```

profile of v0, /device:TPU:25, one launch (start us, length us, event | category | flops | bytes accessed | tf_op | source)
XLA Modules:
  0.0 288.3 jit_solution(11351128227814640421)
XLA Ops:
  9.1 18.3 %all-to-all-start = ((s32[64,1,1]{2,1,0:T(1,128)}), s32[64,1,1]{2,1,0:T(1,128)S(1)}, u32[]{:S(2)}, u32[]{:S(2)}) async-start(s32[64,1,1]{2,1,0:T(1,128)} %copy.16), calls=%async_computation | async-start | bytes 65536 | tf_op jit(solution)/shard_map/all_to_all | solution.py:60
  28.4 3.4 %gather_fusion.5 = bf16[256,1920]{1,0:T(8,128)(2,1)S(1)} fusion(bf16[128,1920]{1,0:T(8,128)(2,1)} %param.10, s32[1024]{0:T(1024)S(1)} %pad_clamp_fusion.4), kind=kCustom, calls=%fused_computation.clone | custom fusion | bytes 1967104 | tf_op jit(solution)/shard_map/jit(_take)/gather | solution.py:56
  31.8 1.2 select_select_fusion.1
  33.1 2.6 all_to_all.25
  35.6 5.2 %all-to-all-done = s32[64,1,1]{2,1,0:T(1,128)S(1)} async-done(((s32[64,1,1]{2,1,0:T(1,128)}), s32[64,1,1]{2,1,0:T(1,128)S(1)}, u32[]{:S(2)}, u32[]{:S(2)}) %all-to-all-start) | async-done | bytes 288 | tf_op jit(solution)/shard_map/all_to_all | solution.py:60
  40.8 9.6 %all-to-all-start.1 = ((bf16[64,4,1920]{2,1,0:T(4,128)(2,1)}), bf16[64,4,1920]{2,1,0:T(4,128)(2,1)}, u32[]{:S(2)}, u32[]{:S(2)}) async-start(bf16[64,4,1920]{2,1,0:T(4,128)(2,1)} %all_to_all.25), calls=%async_computation.1 | async-start | bytes 1966080 | tf_op jit(solution)/shard_map/all_to_all | solution.py:59
  50.7 1.2 reduce
  52.0 1.2 gather_fusion.1
  53.3 45.7 %all-to-all-done.1 = bf16[64,4,1920]{2,1,0:T(4,128)(2,1)} async-done(((bf16[64,4,1920]{2,1,0:T(4,128)(2,1)}), bf16[64,4,1920]{2,1,0:T(4,128)(2,1)}, u32[]{:S(2)}, u32[]{:S(2)}) %all-to-all-start.1) | async-done | bytes 983072 | tf_op jit(solution)/shard_map/all_to_all | solution.py:59
  99.0 1.7 all_to_all.27
  100.7 0.9 gather_fusion.6
  101.6 0.9 broadcast_select_fusion
  102.8 32.6 %all-gather.2.cloned.1.call-done = bf16[1024,1920]{1,0:T(8,128)(2,1)} async-done(((bf16[128,1920]{1,0:T(8,128)(2,1)}), bf16[1024,1920]{1,0:T(8,128)(2,1)}) %all-gather.2.cloned.1.call-update) | async-done | bytes 3932176 | tf_op jit(solution)/shard_map/all_gather | solution.py:70
  135.4 2.8 convert_reduce_fusion
  138.7 1.2 fusion.2
  139.9 9.2 %convolution_convert_fusion = bf16[1024,1920]{1,0:T(8,128)(2,1)} fusion(bf16[1,512,1920]{2,1,0:T(8,128)(2,1)S(1)} %copy-done, bf16[1,512,1920]{2,1,0:T(8,128)(2,1)} %param.14, bf16[1024,1920]{1,0:T(8,128)(2,1)} %all-gather.2.cloned.1.call-done, f32[1920]{0:T(1024)S(1)} %reduce.2, f32[1024]{0:T(1024)S(1)} %add_rsqrt_fusion, f32[1024]{0:T(1024)S(1)} %broadcast_multiply_fusion), kind=kOutput, calls=%fused_computation.20 | convolution fusion | flops 4039376896 | bytes 11812352 | tf_op jit(solution)/shard_map/dot_general | solution.py:36
  149.1 1.9 gather_fusion
  151.0 1.9 gather_fusion.2
  153.4 1.9 gather_fusion.3
  156.0 39.2 %reduce-scatter.2.cloned.1.call-done = bf16[128,1920]{1,0:T(8,128)(2,1)} async-done(((bf16[1024,1920]{1,0:T(8,128)(2,1)}), bf16[128,1920]{1,0:T(8,128)(2,1)}) %reduce-scatter.2.cloned.1.call-update) | async-done | bytes 491536 | tf_op jit(solution)/shard_map/reduce_scatter | solution.py:74
  195.1 3.4 %gather_fusion.7 = bf16[256,1920]{1,0:T(8,128)(2,1)S(1)} fusion(bf16[128,1920]{1,0:T(8,128)(2,1)} %reduce-scatter.2.cloned.1.call-done, s32[1024]{0:T(1024)S(1)} %pad_clamp_fusion.2), kind=kCustom, calls=%fused_computation.2.clone | custom fusion | bytes 1967104 | tf_op jit(solution)/shard_map/jit(_take)/gather | solution.py:82
  198.6 1.2 select_select_fusion
  199.8 1.8 concatenate.6
  201.6 1.6 pad_maximum_fusion
  203.3 14.3 %all-to-all-start.2 = ((bf16[64,4,1921]{2,1,0:T(4,128)(2,1)}), bf16[64,4,1921]{2,1,0:T(4,128)(2,1)S(1)}, u32[]{:S(2)}, u32[]{:S(2)}) async-start(bf16[64,4,1921]{2,1,0:T(4,128)(2,1)} %pad_maximum_fusion), calls=%async_computation.3 | async-start | bytes 2097152 | tf_op jit(solution)/shard_map/all_to_all | solution.py:13
  217.6 55.2 %all-to-all-done.2 = bf16[64,4,1921]{2,1,0:T(4,128)(2,1)S(1)} async-done(((bf16[64,4,1921]{2,1,0:T(4,128)(2,1)}), bf16[64,4,1921]{2,1,0:T(4,128)(2,1)S(1)}, u32[]{:S(2)}, u32[]{:S(2)}) %all-to-all-start.2) | async-done | bytes 983584 | tf_op jit(solution)/shard_map/all_to_all | solution.py:13
  272.8 1.3 all_to_all.29
  274.1 1.3 slice.27
  275.4 0.9 slice_reduce_fusion
  276.4 1.7 gather_fusion.8
  278.1 1.2 gather_fusion.4
  279.3 2.1 add_convert_fusion
  (51 shorter events, 5.8 us)
Async XLA Ops:
  6.5 133.3 %copy-start = (bf16[1,512,1920]{2,1,0:T(8,128)(2,1)S(1)}, bf16[1,512,1920]{2,1,0:T(8,128)(2,1)}, u32[]{:S(2)}) copy-start(bf16[1,512,1920]{2,1,0:T(8,128)(2,1)} %param.15) | copy-start | bytes 5898244
  9.1 31.7 %all-to-all-start = ((s32[64,1,1]{2,1,0:T(1,128)}), s32[64,1,1]{2,1,0:T(1,128)S(1)}, u32[]{:S(2)}, u32[]{:S(2)}) async-start(s32[64,1,1]{2,1,0:T(1,128)} %copy.16), calls=%async_computation | async-start | bytes 65536 | tf_op jit(solution)/shard_map/all_to_all | solution.py:60
  40.8 58.2 %all-to-all-start.1 = ((bf16[64,4,1920]{2,1,0:T(4,128)(2,1)}), bf16[64,4,1920]{2,1,0:T(4,128)(2,1)}, u32[]{:S(2)}, u32[]{:S(2)}) async-start(bf16[64,4,1920]{2,1,0:T(4,128)(2,1)} %all_to_all.25), calls=%async_computation.1 | async-start | bytes 1966080 | tf_op jit(solution)/shard_map/all_to_all | solution.py:59
  50.4 85.0 %all-gather.2.cloned.1.call-start = ((), (), s32[]{:S(2)}) async-start(), calls=%async_computation.4 | async-start | bytes 4423680 | tf_op jit(solution)/shard_map/all_gather | solution.py:70
  53.3 49.5 %copy-start.4 = (f32[1,1920]{1,0:T(1,128)S(1)}, f32[1,1920]{1,0:T(1,128)}, u32[]{:S(2)}) copy-start(f32[1,1920]{1,0:T(1,128)} %param.13) | copy-start | bytes 23044
  102.6 92.6 %reduce-scatter.2.cloned.1.call-start = ((), (), s32[]{:S(2)}) async-start(), calls=%async_computation.5 | async-start | bytes 4423680 | tf_op jit(solution)/shard_map/reduce_scatter | solution.py:74
  135.4 3.3 %copy-start.2 = (bf16[1024,1920]{1,0:T(8,128)(2,1)S(1)}, bf16[1024,1920]{1,0:T(8,128)(2,1)}, u32[]{:S(2)}) copy-start(bf16[1024,1920]{1,0:T(8,128)(2,1)} %all-gather.2.cloned.1.call-done) | copy-start | bytes 11796484
  149.0 4.1 %copy-start.3 = (bf16[128,1920]{1,0:T(8,128)(2,1)S(1)}, bf16[128,1920]{1,0:T(8,128)(2,1)}, u32[]{:S(2)}) copy-start(bf16[128,1920]{1,0:T(8,128)(2,1)} %broadcast_select_fusion) | copy-start | bytes 1474564
  149.1 4.1 %copy-start.5 = (bf16[1,1920]{1,0:T(2,128)(2,1)S(1)}, bf16[1,1920]{1,0:T(2,128)(2,1)}, u32[]{:S(2)}) copy-start(bf16[1,1920]{1,0:T(2,128)(2,1)} %param.12) | copy-start | bytes 11524
  203.3 69.5 %all-to-all-start.2 = ((bf16[64,4,1921]{2,1,0:T(4,128)(2,1)}), bf16[64,4,1921]{2,1,0:T(4,128)(2,1)S(1)}, u32[]{:S(2)}, u32[]{:S(2)}) async-start(bf16[64,4,1921]{2,1,0:T(4,128)(2,1)} %pad_maximum_fusion), calls=%async_computation.3 | async-start | bytes 2097152 | tf_op jit(solution)/shard_map/all_to_all | solution.py:13
  274.1 5.3 %copy-start.1 = (bf16[128,1920]{1,0:T(8,128)(2,1)S(1)}, bf16[128,1920]{1,0:T(8,128)(2,1)}, u32[]{:S(2)}) copy-start(bf16[128,1920]{1,0:T(8,128)(2,1)} %param.10) | copy-start | bytes 1474564
Sparse Core Ops, SparseCore 0:
  102.7 32.6 all-gather.1
  149.2 45.8 reduce-scatter.1
where the time goes:
time: 289 us; the launch traced here: 288 us
  waiting for transfers between devices  178 us (62%)
  starting transfers between devices  42.5 us (15%)
  local copies, waits for them, and re-layouts  29.3 us (10%)
  other arithmetic  15.6 us (5%)
  between operations  13.7 us (5%)
  matrix products  9.41 us (3%)
    all_to_all x1, waiting for transfers between devices, in_one_piece(): lax.all_to_all(both, axis, split_axis=split_dim, concat_axis=concat_dim,...  55.2 us
    all_to_all x1, waiting for transfers between devices, body(): lax.all_to_all(outgoing, 'expert', split_axis=0, concat_axis=0, tiled=True)  45.7 us
    reduce_scatter x1, waiting for transfers between devices, body(): lax.psum_scatter(partial_value.astype(jnp.bfloat16), 'dp', scatter_dimens...  39.2 us
    all_gather x1, waiting for transfers between devices, body(): lax.all_gather(local_rows, 'dp', axis=0, tiled=True)  32.6 us
    all_to_all x1, starting transfers between devices, body(): lax.all_to_all(send_counts, 'expert', split_axis=0, concat_axis=0, tiled=...  18.3 us
    all_to_all x1, starting transfers between devices, in_one_piece(): lax.all_to_all(both, axis, split_axis=split_dim, concat_axis=concat_dim,...  14.3 us
    all_to_all x1, starting transfers between devices, body(): lax.all_to_all(outgoing, 'expert', split_axis=0, concat_axis=0, tiled=True)  9.56 us
    dot_general x1, matrix products, expert_rows(): return jnp.dot(hidden, outer_mat, preferred_element_type=jnp.float32)  9.17 us
  transfers between devices with their start and end apart: 5, of which 5 were waited for; matrix products, arithmetic and copies ran while one was open for 5% of the time, Pallas kernels for 0%

commit v1 on v0

v1 whole, which is shorter than its diff:
```python
import functools

import jax
import jax.numpy as jnp
from jax import lax
from jax.experimental import pallas as pl
from jax.experimental.pallas import tpu as pltpu
from jax.sharding import PartitionSpec as P

MESH = pl.DeviceIdType.MESH
EPS = 1e-05
NZ, NX, NY = 16, 4, 4
CAP = 4
CHUNKS = ((1, 15, 7, 9), (2, 14, 6, 10), (3, 13, 5, 11), (4, 12, 8, 0))
NCH = len(CHUNKS)
PER = 16
XS = (1, 2, 3, 0)
OFFS = tuple((dz, dx) for c in CHUNKS for dz in c for dx in XS)
ROWS = PER * CAP
F32, BF16 = jnp.float32, jnp.bfloat16


def kernel(
    tok_hbm, asg_ref, cen_ref, gain_ref, w1_hbm, w2_hbm, out_ref,
    tok, w1, w2, snd, rcv, grp, psend, precv, part, qs, rq, ret, back, gates,
    lsem, dsend, drecv, asend, arecv, psem_s, psem_r, qsem_s, qsem_r, rsend, rrecv,
):
    dp, e = lax.axis_index("dp"), lax.axis_index("expert")
    y, c = dp // 2, lax.rem(dp, 2)
    z, x = e // NX, lax.rem(e, NX)
    d_model = tok.shape[1]

    tok_cp = pltpu.make_async_copy(tok_hbm, tok, lsem.at[0])
    w1_cp = pltpu.make_async_copy(w1_hbm.at[0], w1, lsem.at[1])
    w2_cp = pltpu.make_async_copy(w2_hbm.at[0], w2, lsem.at[2])
    tok_cp.start()
    w1_cp.start()
    w2_cp.start()

    def chip(step):
        return lax.rem(y + step, NY) * 2 + c

    partner = (y * 2 + (1 - c), e)
    dirf = 1 + 2 * c
    dirb = 3 - 2 * c
    ahead, behind = (chip(dirf), e), (chip(dirb), e)

    def to(dz, dx):
        return (dp, lax.rem(z + dz, NZ) * NX + lax.rem(x + dx, NX))

    bar = pltpu.get_barrier_semaphore()
    peers = [to(dz, dx) for dz, dx in OFFS[:-1]] + [partner, ahead, behind]
    for peer in peers:
        pl.semaphore_signal(bar, inc=1, device_id=peer, device_id_type=MESH)

    n_tok = tok.shape[0]
    a_row = asg_ref[...]
    ri = lax.broadcasted_iota(jnp.int32, (n_tok, n_tok), 0)
    ci = lax.broadcasted_iota(jnp.int32, (n_tok, n_tok), 1)
    a_lane = jnp.broadcast_to(a_row, (n_tok, n_tok))
    a_col = jnp.sum(jnp.where(ri == ci, a_lane, 0), axis=1, keepdims=True)
    same = a_lane == a_col
    pos_row = jnp.sum(jnp.where(same & (ri < ci), 1, 0), axis=0, keepdims=True)
    pos_col = jnp.sum(jnp.where(same & (ci < ri), 1, 0), axis=1, keepdims=True)

    def row_of(a, pos):
        dz = (a // NX - z + NZ) & (NZ - 1)
        dx = (a - z * NX - x + NZ * NX) & (NX - 1)
        kz = jnp.zeros_like(a)
        for i, v in enumerate(v for ch in CHUNKS for v in ch):
            kz = jnp.where(dz == v, i, kz)
        kx = (dx + NX - 1) & (NX - 1)
        return (kz * NX + kx) * CAP + pos


    row_r = row_of(a_row, pos_row)
    row_c = row_of(a_col, pos_col)
    n_slot = NCH * ROWS
    pick = jnp.where(
        lax.broadcasted_iota(jnp.int32, (n_slot, n_tok), 0) == row_r, 1.0, 0.0
    ).astype(BF16)
    tok_cp.wait()
    slots = jnp.dot(pick, tok[...], preferred_element_type=F32)
    snd[...] = slots.reshape(NCH * PER, CAP, d_model).astype(BF16)

    pl.semaphore_wait(bar, len(peers))

    def dispatch(k):
        return pltpu.make_async_remote_copy(
            src_ref=snd.at[k],
            dst_ref=rcv.at[k],
            send_sem=dsend,
            recv_sem=drecv.at[k // PER],
            device_id=to(*OFFS[k]),
            device_id_type=MESH,
        )

    last = NCH * PER - 1
    for k in range(last):
        dispatch(k).start()
    own_in = pltpu.make_async_copy(snd.at[last], rcv.at[last], lsem.at[3])
    own_in.start()

    def all_of(ref, first, count, sem):
        view = ref.at[pl.ds(first, count)]
        return pltpu.make_async_copy(view, view, sem)

    def n_remote(j):
        return PER - 1 if j == NCH - 1 else PER

    def block(j, s, r):
        return grp.at[j, pl.ds((s * NY + r) * ROWS, ROWS)]

    def remote(src, dst, ssem, rsem, dev):
        return pltpu.make_async_remote_copy(
            src_ref=src, dst_ref=dst, send_sem=ssem, recv_sem=rsem,
            device_id=dev, device_id_type=MESH,
        )

    rf, rb = 1 + 2 * c, 3 - 2 * c

    def ag_ahead(j):
        return remote(block(j, 0, 0), block(j, 0, rf), asend.at[j, 0], arecv.at[j, rf], ahead)

    def ag_behind(j):
        return remote(block(j, 0, 0), block(j, 0, rb), asend.at[j, 1], arecv.at[j, rb], behind)

    def ag_on(j):
        return remote(block(j, 0, rf), block(j, 0, 2), asend.at[j, 2], arecv.at[j, 2], ahead)

    def ag_side(j, r):
        return remote(
            block(j, 0, r), block(j, 1, r), asend.at[j, 4 + r], arecv.at[j, NY + r], partner
        )

    def arrived(j, s, r):
        view = block(j, s, r)
        pltpu.make_async_copy(view, view, arecv.at[j, s * NY + r]).wait()

    def stage_a(j):
        all_of(rcv, j * PER, n_remote(j), drecv.at[j]).wait()
        if j == NCH - 1:
            own_in.wait()
        v = rcv[pl.ds(j * PER, PER)].astype(F32).reshape(ROWS, d_model)
        center = jnp.mean(v, axis=1, keepdims=True)
        dev = v - center
        spread = jnp.mean(dev * dev, axis=1, keepdims=True)
        normed = (dev * lax.rsqrt(spread + EPS) * gain_ref[...]).astype(BF16)
        grp[j, pl.ds(0, ROWS)] = normed
        ag_ahead(j).start()
        ag_behind(j).start()
        ag_side(j, 0).start()
        score = jnp.sum(v * cen_ref[...].astype(F32), axis=1, keepdims=True)
        gate = (1.0 / (1.0 + jnp.exp(-score))).astype(BF16).astype(F32)
        gates[j] = jnp.broadcast_to(gate, (ROWS, 128))

    def stage_b(j):
        arrived(j, 0, rf)
        ag_on(j).start()
        arrived(j, 0, rb)
        ag_side(j, 1).start()
        ag_side(j, 3).start()

    def stage_c(j):
        arrived(j, 0, 2)
        ag_side(j, 2).start()

    def mlp(rows):
        act = lax.dot_general(
            rows, w1[...], (((1,), (1,)), ((), ())), preferred_element_type=F32
        )
        hidden = jnp.maximum(act, 0.0).astype(BF16)
        return jnp.dot(hidden, w2[...], preferred_element_type=F32)

    half = NY * ROWS

    def swap(j):
        return remote(psend.at[j], precv.at[j], psem_s.at[j], psem_r.at[j], partner)

    def stage_d(j):
        if j == 0:
            w1_cp.wait()
            w2_cp.wait()
        for r in range(NY):
            arrived(j, 1, r)
        psend[j] = mlp(grp[j, pl.ds(half, half)]).astype(BF16)
        swap(j).start()
        part[j % 2] = mlp(grp[j, pl.ds(0, half)])

    rc, rd = 3 - 2 * c, 1 + 2 * c

    def q_far(j):
        return remote(qs.at[j, 0], rq.at[j, 0], qsem_s.at[j, 0], qsem_r.at[j, 0], ahead)

    def q_on(j):
        return remote(qs.at[j, 1], rq.at[j, 1], qsem_s.at[j, 1], qsem_r.at[j, 1], ahead)

    def q_near(j):
        return remote(qs.at[j, 2], rq.at[j, 2], qsem_s.at[j, 2], qsem_r.at[j, 2], behind)

    def q_wait(j, i):
        view = rq.at[j, i]
        pltpu.make_async_copy(view, view, qsem_r.at[j, i]).wait()

    def rows_of(r):
        return pl.ds(pl.multiple_of(r * ROWS, ROWS), ROWS)

    def pair_sum(j, r):
        return part[j % 2, rows_of(r)] + precv[j, rows_of(r)].astype(F32)

    def stage_e(j):
        view = precv.at[j]
        pltpu.make_async_copy(view, view, psem_r.at[j]).wait()
        qs[j, 0] = pair_sum(j, 2).astype(BF16)
        q_far(j).start()
        qs[j, 2] = pair_sum(j, rd).astype(BF16)
        q_near(j).start()

    def stage_f(j):
        q_wait(j, 0)
        qs[j, 1] = (pair_sum(j, rc) + rq[j, 0].astype(F32)).astype(BF16)
        q_on(j).start()

    def give_back(k):
        dz, dx = OFFS[k]
        return pltpu.make_async_remote_copy(
            src_ref=ret.at[k],
            dst_ref=back.at[k],
            send_sem=rsend,
            recv_sem=rrecv.at[k // PER],
            device_id=to(NZ - dz, NX - dx),
            device_id_type=MESH,
        )

    own_out = pltpu.make_async_copy(ret.at[last], back.at[last], lsem.at[4])

    def stage_g(j):
        q_wait(j, 2)
        total = pair_sum(j, 0) + rq[j, 2].astype(F32)
        q_wait(j, 1)
        total = total + rq[j, 1].astype(F32)
        scaled = total * gates[j][:, :1]
        ret[pl.ds(j * PER, PER)] = scaled.reshape(PER, CAP, d_model).astype(BF16)
        for k in range(j * PER, j * PER + n_remote(j)):
            give_back(k).start()
        if j == NCH - 1:
            own_out.start()

    for t in range(NCH + 2):
        for stage, j in (
            (stage_a, t), (stage_c, t - 1), (stage_f, t - 2), (stage_d, t - 1),
            (stage_g, t - 2), (stage_b, t), (stage_e, t - 1),
        ):
            if 0 <= j < NCH:
                stage(j)

    acc = tok[...].astype(F32)
    for j in range(NCH):
        all_of(back, j * PER, n_remote(j), rrecv.at[j]).wait()
        if j == NCH - 1:
            own_out.wait()
        rows = back[pl.ds(j * PER, PER)].astype(F32).reshape(ROWS, d_model).astype(BF16)
        choose = jnp.where(
            lax.broadcasted_iota(jnp.int32, (n_tok, ROWS), 1) + j * ROWS == row_c, 1.0, 0.0
        ).astype(BF16)
        acc = acc + jnp.dot(choose, rows, preferred_element_type=F32)
    out_ref[...] = acc.astype(BF16)

    all_of(snd, 0, last, dsend).wait()
    all_of(ret, 0, last, rsend).wait()
    for j in range(NCH):
        ag_ahead(j).wait_send()
        ag_behind(j).wait_send()
        ag_on(j).wait_send()
        for r in range(NY):
            ag_side(j, r).wait_send()
        swap(j).wait_send()
        q_far(j).wait_send()
        q_on(j).wait_send()
        q_near(j).wait_send()


def body(tokens, assignment, centroids, norm_gain, inner_weight, outer_weight):
    n_tok, d = tokens.shape
    hidden = inner_weight.shape[1]
    half = NY * ROWS
    vmem, anyspace = pltpu.VMEM, pl.ANY
    dma = pltpu.SemaphoreType.DMA
    return pl.pallas_call(
        kernel,
        out_shape=jax.ShapeDtypeStruct((n_tok, d), BF16),
        in_specs=[
            pl.BlockSpec(memory_space=anyspace),
            pl.BlockSpec(memory_space=vmem),
            pl.BlockSpec(memory_space=vmem),
            pl.BlockSpec(memory_space=vmem),
            pl.BlockSpec(memory_space=anyspace),
            pl.BlockSpec(memory_space=anyspace),
        ],
        out_specs=pl.BlockSpec(memory_space=vmem),
        scratch_shapes=[
            vmem((n_tok, d), BF16),
            vmem((hidden, d), BF16),
            vmem((hidden, d), BF16),
            vmem((NCH * PER, CAP, d), BF16),
            vmem((NCH * PER, CAP, d), BF16),
            vmem((NCH, 2 * half, d), BF16),
            vmem((NCH, half, d), BF16),
            vmem((NCH, half, d), BF16),
            vmem((2, half, d), F32),
            vmem((NCH, 3, ROWS, d), BF16),
            vmem((NCH, 3, ROWS, d), BF16),
            vmem((NCH * PER, CAP, d), BF16),
            vmem((NCH * PER, CAP, d), BF16),
            vmem((NCH, ROWS, 128), F32),
            dma((5,)),
            dma,
            dma((NCH,)),
            dma((NCH, 8)),
            dma((NCH, 8)),
            dma((NCH,)),
            dma((NCH,)),
            dma((NCH, 3)),
            dma((NCH, 3)),
            dma,
            dma((NCH,)),
        ],
        compiler_params=pltpu.CompilerParams(
            collective_id=0, has_side_effects=True, vmem_limit_bytes=60 * 2**20
        ),
    )(tokens, assignment.reshape(1, n_tok), centroids, norm_gain, inner_weight, outer_weight)


def solution(mesh):
    in_specs = (
        P(("dp", "expert"), None),
        P(("dp", "expert")),
        P("expert", None),
        P("expert", None),
        P("expert", "dp", None),
        P("expert", "dp", None),
    )
    out_specs = P(("dp", "expert"), None)
    return jax.shard_map(body, mesh=mesh, in_specs=in_specs, out_specs=out_specs, check_vma=False)
```

time: 289 us -> 138 us (0.48)
  the two profiles are of different devices: /device:TPU:25 before, /device:TPU:40 now
where the time goes in v1:
time: 138 us
  Pallas kernels  136 us (99%)
  local copies, waits for them, and re-layouts  1.84 us (1%)
    pallas_call x1, Pallas kernels, body(): pl.pallas_call(kernel, out_shape=jax.ShapeDtypeStruct((n_tok, d), BF16),...  136 us

profile of v1, /device:TPU:40, one launch (start us, length us, event | category | flops | bytes accessed | tf_op | source)
XLA Modules:
  0.0 138.3 jit_solution(7309554236535834233)
XLA Ops:
  0.0 136.4 %shard_map.64 = bf16[128,1920]{1,0:T(8,128)(2,1)} custom-call(bf16[128,1920]{1,0:T(8,128)(2,1)} %tok_hbm.1, s32[1,128]{1,0:T(1,128)} %bitcast.1, bf16[1,1920]{1,0:T(2,128)(2,1)} %cen_ref.1, f32[1,1920]{1,0:T(1,128)} %gain_ref.1, bf16[1,512,1920]{2,1,0:T(8,128)(2,1)} %w1_hbm.1, bf16[1,512,1920]{2,1,0:T(8,128)(2,1)} %w2_hbm.1), custom_call_target="tpu_custom_call" | custom-call | tf_op jit(solution)/shard_map/pallas_call | solution.py:289
  136.4 1.8 %copy.8 = bf16[128,1920]{1,0:T(8,128)(2,1)} copy(bf16[128,1920]{1,0:T(8,128)(2,1)} %shard_map.64) | data formatting | bytes 983040

commit v2 on v1

--- a/solution.py
+++ b/solution.py
@@ -11,9 +11,11 @@
 EPS = 1e-05
 NZ, NX, NY = 16, 4, 4
 CAP = 4
-CHUNKS = ((1, 15, 7, 9), (2, 14, 6, 10), (3, 13, 5, 11), (4, 12, 8, 0))
+CHUNKS = ((1, 15), (3, 13), (5, 11), (7, 9), (6, 10), (4, 12), (2, 14), (8, 0))
 NCH = len(CHUNKS)
-PER = 16
+PER = NX * len(CHUNKS[0])
+LAGS = dict(a=0.0, b=0.9, c=1.6, d=2.3, e=3.2, f=4.0, g=4.9)
+NPART = 5
 XS = (1, 2, 3, 0)
 OFFS = tuple((dz, dx) for c in CHUNKS for dz in c for dx in XS)
 ROWS = PER * CAP
@@ -185,7 +187,7 @@
             arrived(j, 1, r)
         psend[j] = mlp(grp[j, pl.ds(half, half)]).astype(BF16)
         swap(j).start()
-        part[j % 2] = mlp(grp[j, pl.ds(0, half)])
+        part[j % NPART] = mlp(grp[j, pl.ds(0, half)])
 
     rc, rd = 3 - 2 * c, 1 + 2 * c
 
@@ -206,7 +208,7 @@
         return pl.ds(pl.multiple_of(r * ROWS, ROWS), ROWS)
 
     def pair_sum(j, r):
-        return part[j % 2, rows_of(r)] + precv[j, rows_of(r)].astype(F32)
+        return part[j % NPART, rows_of(r)] + precv[j, rows_of(r)].astype(F32)
 
     def stage_e(j):
         view = precv.at[j]
@@ -246,13 +248,11 @@
         if j == NCH - 1:
             own_out.start()
 
-    for t in range(NCH + 2):
-        for stage, j in (
-            (stage_a, t), (stage_c, t - 1), (stage_f, t - 2), (stage_d, t - 1),
-            (stage_g, t - 2), (stage_b, t), (stage_e, t - 1),
-        ):
-            if 0 <= j < NCH:
-                stage(j)
+    stages = dict(
+        a=stage_a, b=stage_b, c=stage_c, d=stage_d, e=stage_e, f=stage_f, g=stage_g
+    )
+    for _, name, j in sorted((j + LAGS[n], n, j) for n in stages for j in range(NCH)):
+        stages[name](j)
 
     acc = tok[...].astype(F32)
     for j in range(NCH):
@@ -307,7 +307,7 @@
             vmem((NCH, 2 * half, d), BF16),
             vmem((NCH, half, d), BF16),
             vmem((NCH, half, d), BF16),
-            vmem((2, half, d), F32),
+            vmem((NPART, half, d), F32),
             vmem((NCH, 3, ROWS, d), BF16),
             vmem((NCH, 3, ROWS, d), BF16),
             vmem((NCH * PER, CAP, d), BF16),

time: 138 us -> 124 us (0.90)
  the two profiles are of different devices: /device:TPU:40 before, /device:TPU:25 now
where the time goes in v2:
time: 124 us; the launch traced here: 122 us
  Pallas kernels  121 us (98%)
  local copies, waits for them, and re-layouts  1.84 us (1%)
    pallas_call x1, Pallas kernels, body(): pl.pallas_call(kernel, out_shape=jax.ShapeDtypeStruct((n_tok, d), BF16),...  121 us

profile of v2, /device:TPU:25, one launch (start us, length us, event | category | flops | bytes accessed | tf_op | source)
XLA Modules:
  0.0 122.4 jit_solution(6594985607073411728)
XLA Ops:
  0.0 120.6 %shard_map.64 = bf16[128,1920]{1,0:T(8,128)(2,1)} custom-call(bf16[128,1920]{1,0:T(8,128)(2,1)} %tok_hbm.1, s32[1,128]{1,0:T(1,128)} %bitcast.1, bf16[1,1920]{1,0:T(2,128)(2,1)} %cen_ref.1, f32[1,1920]{1,0:T(1,128)} %gain_ref.1, bf16[1,512,1920]{2,1,0:T(8,128)(2,1)} %w1_hbm.1, bf16[1,512,1920]{2,1,0:T(8,128)(2,1)} %w2_hbm.1), custom_call_target="tpu_custom_call" | custom-call | tf_op jit(solution)/shard_map/pallas_call | solution.py:289
  120.6 1.8 %copy.8 = bf16[128,1920]{1,0:T(8,128)(2,1)} copy(bf16[128,1920]{1,0:T(8,128)(2,1)} %shard_map.64) | data formatting | bytes 983040

commit v3 on v2

--- a/solution.py
+++ b/solution.py
@@ -11,13 +11,14 @@
 EPS = 1e-05
 NZ, NX, NY = 16, 4, 4
 CAP = 4
-CHUNKS = ((1, 15), (3, 13), (5, 11), (7, 9), (6, 10), (4, 12), (2, 14), (8, 0))
+CHUNKS = ((1, 15), (4, 12), (7, 9), (3, 13), (8, 0), (5, 11), (6, 10), (2, 14))
 NCH = len(CHUNKS)
 PER = NX * len(CHUNKS[0])
 LAGS = dict(a=0.0, b=0.9, c=1.6, d=2.3, e=3.2, f=4.0, g=4.9)
 NPART = 5
 XS = (1, 2, 3, 0)
 OFFS = tuple((dz, dx) for c in CHUNKS for dz in c for dx in XS)
+OWN = OFFS.index((0, 0))
 ROWS = PER * CAP
 F32, BF16 = jnp.float32, jnp.bfloat16
 
@@ -51,7 +52,7 @@
         return (dp, lax.rem(z + dz, NZ) * NX + lax.rem(x + dx, NX))
 
     bar = pltpu.get_barrier_semaphore()
-    peers = [to(dz, dx) for dz, dx in OFFS[:-1]] + [partner, ahead, behind]
+    peers = [to(*o) for o in OFFS if o != (0, 0)] + [partner, ahead, behind]
     for peer in peers:
         pl.semaphore_signal(bar, inc=1, device_id=peer, device_id_type=MESH)
 
@@ -97,10 +98,11 @@
             device_id_type=MESH,
         )
 
-    last = NCH * PER - 1
-    for k in range(last):
-        dispatch(k).start()
-    own_in = pltpu.make_async_copy(snd.at[last], rcv.at[last], lsem.at[3])
+    remotes = NCH * PER - 1
+    for k in range(NCH * PER):
+        if k != OWN:
+            dispatch(k).start()
+    own_in = pltpu.make_async_copy(snd.at[OWN], rcv.at[OWN], lsem.at[3])
     own_in.start()
 
     def all_of(ref, first, count, sem):
@@ -108,7 +110,7 @@
         return pltpu.make_async_copy(view, view, sem)
 
     def n_remote(j):
-        return PER - 1 if j == NCH - 1 else PER
+        return PER - 1 if j == OWN // PER else PER
 
     def block(j, s, r):
         return grp.at[j, pl.ds((s * NY + r) * ROWS, ROWS)]
@@ -141,7 +143,7 @@
 
     def stage_a(j):
         all_of(rcv, j * PER, n_remote(j), drecv.at[j]).wait()
-        if j == NCH - 1:
+        if j == OWN // PER:
             own_in.wait()
         v = rcv[pl.ds(j * PER, PER)].astype(F32).reshape(ROWS, d_model)
         center = jnp.mean(v, axis=1, keepdims=True)
@@ -185,9 +187,10 @@
             w2_cp.wait()
         for r in range(NY):
             arrived(j, 1, r)
-        psend[j] = mlp(grp[j, pl.ds(half, half)]).astype(BF16)
+        both = mlp(grp[j])
+        psend[j] = both[half:].astype(BF16)
         swap(j).start()
-        part[j % NPART] = mlp(grp[j, pl.ds(0, half)])
+        part[j % NPART] = both[:half]
 
     rc, rd = 3 - 2 * c, 1 + 2 * c
 
@@ -234,7 +237,7 @@
             device_id_type=MESH,
         )
 
-    own_out = pltpu.make_async_copy(ret.at[last], back.at[last], lsem.at[4])
+    own_out = pltpu.make_async_copy(ret.at[OWN], back.at[OWN], lsem.at[4])
 
     def stage_g(j):
         q_wait(j, 2)
@@ -245,7 +248,7 @@
         ret[pl.ds(j * PER, PER)] = scaled.reshape(PER, CAP, d_model).astype(BF16)
         for k in range(j * PER, j * PER + n_remote(j)):
             give_back(k).start()
-        if j == NCH - 1:
+        if j == OWN // PER:
             own_out.start()
 
     stages = dict(
@@ -257,7 +260,7 @@
     acc = tok[...].astype(F32)
     for j in range(NCH):
         all_of(back, j * PER, n_remote(j), rrecv.at[j]).wait()
-        if j == NCH - 1:
+        if j == OWN // PER:
             own_out.wait()
         rows = back[pl.ds(j * PER, PER)].astype(F32).reshape(ROWS, d_model).astype(BF16)
         choose = jnp.where(
@@ -266,8 +269,8 @@
         acc = acc + jnp.dot(choose, rows, preferred_element_type=F32)
     out_ref[...] = acc.astype(BF16)
 
-    all_of(snd, 0, last, dsend).wait()
-    all_of(ret, 0, last, rsend).wait()
+    all_of(snd, 0, remotes, dsend).wait()
+    all_of(ret, 0, remotes, rsend).wait()
     for j in range(NCH):
         ag_ahead(j).wait_send()
         ag_behind(j).wait_send()

time: 124 us -> 123 us (level)
  the two profiles are of different devices: /device:TPU:25 before, /device:TPU:8 now
where the time goes in v3:
time: 123 us
  Pallas kernels  121 us (98%)
  local copies, waits for them, and re-layouts  1.84 us (1%)
    pallas_call x1, Pallas kernels, body(): pl.pallas_call(kernel, out_shape=jax.ShapeDtypeStruct((n_tok, d), BF16),...  121 us

profile of v3, /device:TPU:8, one launch (start us, length us, event | category | flops | bytes accessed | tf_op | source)
XLA Modules:
  0.0 123.2 jit_solution(16242189194885299477)
XLA Ops:
  0.0 121.4 %shard_map.64 = bf16[128,1920]{1,0:T(8,128)(2,1)} custom-call(bf16[128,1920]{1,0:T(8,128)(2,1)} %tok_hbm.1, s32[1,128]{1,0:T(1,128)} %bitcast.1, bf16[1,1920]{1,0:T(2,128)(2,1)} %cen_ref.1, f32[1,1920]{1,0:T(1,128)} %gain_ref.1, bf16[1,512,1920]{2,1,0:T(8,128)(2,1)} %w1_hbm.1, bf16[1,512,1920]{2,1,0:T(8,128)(2,1)} %w2_hbm.1), custom_call_target="tpu_custom_call" | custom-call | tf_op jit(solution)/shard_map/pallas_call | solution.py:292
  121.4 1.8 %copy.8 = bf16[128,1920]{1,0:T(8,128)(2,1)} copy(bf16[128,1920]{1,0:T(8,128)(2,1)} %shard_map.64) | data formatting | bytes 983040

commit v4 on v3

--- a/solution.py
+++ b/solution.py
@@ -11,7 +11,7 @@
 EPS = 1e-05
 NZ, NX, NY = 16, 4, 4
 CAP = 4
-CHUNKS = ((1, 15), (4, 12), (7, 9), (3, 13), (8, 0), (5, 11), (6, 10), (2, 14))
+CHUNKS = ((1, 15), (4, 12), (7, 9), (5, 11), (8, 0), (6, 10), (3, 13), (2, 14))
 NCH = len(CHUNKS)
 PER = NX * len(CHUNKS[0])
 LAGS = dict(a=0.0, b=0.9, c=1.6, d=2.3, e=3.2, f=4.0, g=4.9)

time: 123 us -> 123 us (level)
  the two profiles are of different devices: /device:TPU:8 before, /device:TPU:32 now
where the time goes in v4:
time: 123 us
  Pallas kernels  121 us (98%)
  local copies, waits for them, and re-layouts  1.84 us (1%)
    pallas_call x1, Pallas kernels, body(): pl.pallas_call(kernel, out_shape=jax.ShapeDtypeStruct((n_tok, d), BF16),...  121 us

profile of v4, /device:TPU:32, one launch (start us, length us, event | category | flops | bytes accessed | tf_op | source)
XLA Modules:
  0.0 122.6 jit_solution(5461472608495821924)
XLA Ops:
  0.0 120.8 %shard_map.64 = bf16[128,1920]{1,0:T(8,128)(2,1)} custom-call(bf16[128,1920]{1,0:T(8,128)(2,1)} %tok_hbm.1, s32[1,128]{1,0:T(1,128)} %bitcast.1, bf16[1,1920]{1,0:T(2,128)(2,1)} %cen_ref.1, f32[1,1920]{1,0:T(1,128)} %gain_ref.1, bf16[1,512,1920]{2,1,0:T(8,128)(2,1)} %w1_hbm.1, bf16[1,512,1920]{2,1,0:T(8,128)(2,1)} %w2_hbm.1), custom_call_target="tpu_custom_call" | custom-call | tf_op jit(solution)/shard_map/pallas_call | solution.py:292
  120.8 1.8 %copy.8 = bf16[128,1920]{1,0:T(8,128)(2,1)} copy(bf16[128,1920]{1,0:T(8,128)(2,1)} %shard_map.64) | data formatting | bytes 983040
